TPU v7x, 32 devices: a whole 2x2x4 slice. The times are simulated.
32 devices in a mesh: dp: 8 (over y, x, core), mp: 4 (over z).
Axes of the slice: x: 2, y: 2, z: 4, core: 2. Of those that a mesh axis runs over, the one named last changes fastest.
Arguments:
- train_acts: bfloat16 [4096, 2560], P('dp'), may hold values from -6 to 6
- train_grads: bfloat16 [4096, 2560], P('dp'), may hold values from -6 to 6
- lengths: int32 [32], P('dp'), may hold values from 1 to 256, as said below
- query_acts: bfloat16 [128, 2560], replicated, may hold values from -6 to 6
- query_grads: bfloat16 [128, 2560], replicated, may hold values from -0.0059814453 to 0.0059814453
- basis_in: bfloat16 [2560, 2560], P(None, 'mp'), may hold values from -0.125 to 0.125
- basis_out: bfloat16 [2560, 2560], P(None, 'mp'), may hold values from -0.125 to 0.125
Outputs:
- scores: float32 [1, 32], P(None, 'dp')
Inputs may be any that keep to these rules, and one draw needn't show every extreme that they name: The 4 lengths of one index of dp sum to at most 512; in every draw some index's sequences fill all 512 rows and one of them has exactly 256 tokens.
All inputs are finite; a program needn't handle non-finite values.
Results may differ from a plain program's by a relative error of at most 0.0045.
Values may be sent and summed in bfloat16 or wider, within the bound.
A program may use at most 128 MiB of HBM per device.

v0:
```python
import jax
import jax.numpy as jnp
from jax import lax
from jax.sharding import PartitionSpec as P

QUERIES = 1
QLEN = 128
damping_ratio = 0.1


def rotate(values, basis):
    return jnp.dot(values, basis, preferred_element_type=jnp.float32).astype(jnp.bfloat16)


def shards(train_acts, train_grads, lengths, query_acts, query_grads, basis_in, basis_out):
    capacity = train_acts.shape[0]
    window = capacity // 2
    slot_count = lengths.shape[0]
    acts_block = rotate(train_acts, basis_in)
    query_block = rotate(query_acts, basis_in)
    acts_rot, query_rot = (
        lax.all_gather(acts_block, "mp", axis=1, tiled=True),
        lax.all_gather(query_block, "mp", axis=1, tiled=True),
    )
    grads_rot = rotate(train_grads, basis_out)
    query_grot = rotate(query_grads, basis_out).reshape(QUERIES, QLEN, -1)
    finish = jnp.cumsum(lengths)
    starts = finish - lengths
    position = jnp.arange(window, dtype=jnp.int32)
    curvature_local = jnp.zeros((grads_rot.shape[1], acts_rot.shape[1]), jnp.float32)
    stored_list = []
    for slot in range(slot_count):
        begin = jnp.minimum(starts[slot], capacity - window)
        grads_win = lax.dynamic_slice_in_dim(grads_rot, begin, window, 0)
        acts_win = lax.dynamic_slice_in_dim(acts_rot, begin, window, 0)
        inside = (position + begin >= starts[slot]) & (position + begin < finish[slot])
        grads_win = jnp.where(inside[:, None], grads_win, jnp.zeros_like(grads_win))
        product = lax.dot_general(
            grads_win, acts_win, (((0,), (0,)), ((), ())), preferred_element_type=jnp.float32
        )
        curvature_local = curvature_local + product * product
        stored_list.append(product.astype(jnp.bfloat16))
    stored = jnp.stack(stored_list)
    inverse_count = 1.0 / (slot_count * lax.axis_size("dp"))
    query_full = query_rot.reshape(QUERIES, QLEN, -1)
    curvature = lax.psum(curvature_local, "dp") * inverse_count
    grand_total = lax.psum(jnp.sum(curvature), "mp")
    damping = damping_ratio * grand_total / (curvature.size * lax.axis_size("mp"))
    local_grad = jnp.einsum(
        "qti,qtj->qij", query_grot, query_full, preferred_element_type=jnp.float32
    )
    precond = (local_grad / (curvature + damping)).astype(jnp.bfloat16)
    partial_value = jnp.einsum("qik,sik->qs", precond, stored, preferred_element_type=jnp.float32)
    return lax.psum(partial_value, "mp")


def solution(mesh):
    return jax.shard_map(
        shards,
        mesh=mesh,
        in_specs=(P("dp", None), P("dp", None), P("dp"), P(), P(), P(None, "mp"), P(None, "mp")),
        out_specs=P(None, "dp"),
        check_vma=False,
    )
```

profile of v0, /device:TPU:0, one launch (start us, length us, event | category | flops | bytes accessed | tf_op | source)
XLA Modules:
  0.0 276.5 jit_solution(13242700860598171906)
XLA Ops:
  6.5 0.0 copy-start
  6.5 0.0 all-gather.2.cloned.1.call-start
  6.5 5.9 %convolution_convert_fusion = bf16[512,640]{1,0:T(8,128)(2,1)} fusion(bf16[512,2560]{1,0:T(8,128)(2,1)} %param.7, bf16[2560,640]{1,0:T(8,128)(2,1)} %param.12), kind=kOutput, calls=%fused_computation.12 | convolution fusion | flops 1678049280 | bytes 6553600 | tf_op jit(solution)/shard_map/dot_general | solution.py:12
  12.4 0.0 all-gather.2.cloned.1.call-update
  12.5 0.0 all-reduce.2.cloned.1.call-start
  12.5 0.0 copy-done.5
  12.5 0.2 reduce-window.4
  12.7 0.6 fusion.42
  15.9 0.6 fusion.41
  16.5 1.2 compare_and_fusion.1
  17.7 1.3 compare_and_fusion.2
  19.0 1.3 compare_and_fusion
  20.2 1.3 compare_and_fusion.3
  21.5 0.0 copy-done
  21.5 5.0 %convolution_convert_fusion.1 = bf16[512,640]{1,0:T(8,128)(2,1)} fusion(bf16[512,2560]{1,0:T(8,128)(2,1)} %param.8, bf16[2560,640]{1,0:T(8,128)(2,1)S(1)} %copy-done), kind=kOutput, calls=%fused_computation.13 | convolution fusion | flops 1678049280 | bytes 6553600 | tf_op jit(solution)/shard_map/dot_general | solution.py:12
  26.5 43.4 %all-gather.2.cloned.1.call-done = bf16[512,2560]{1,0:T(8,128)(2,1)} async-done(((bf16[512,640]{1,0:T(8,128)(2,1)}), bf16[512,2560]{1,0:T(8,128)(2,1)}) %all-gather.2.cloned.1.call-update) | async-done | bytes 2621456 | tf_op jit(solution)/shard_map/all_gather | solution.py:22
  69.9 2.7 fusion.6
  72.7 0.0 copy-done.3
  72.7 0.0 copy-done.4
  72.7 3.9 %fusion.8 = f32[640,2560]{1,0:T(8,128)} fusion(bf16[512,2560]{1,0:T(8,128)(2,1)S(1)} %copy-done.3, s32[]{:T(128)S(6)} %select_n.31, bf16[512,640]{1,0:T(8,128)(2,1)S(1)} %copy-done.4, pred[256]{0:T(512)(128)(4,1)S(1)} %compare_and_fusion.2), kind=kOutput, calls=%fused_computation.18 | convolution fusion | flops 839024640 | bytes 8193536 | tf_op jit(solution)/shard_map/dot_general | solution.py:38
  76.6 3.9 %fusion.4 = f32[640,2560]{1,0:T(8,128)} fusion(bf16[512,2560]{1,0:T(8,128)(2,1)S(1)} %copy-done.3, s32[]{:T(128)S(6)} %select_n.35, bf16[512,640]{1,0:T(8,128)(2,1)S(1)} %copy-done.4, pred[256]{0:T(512)(128)(4,1)S(1)} %compare_and_fusion), kind=kOutput, calls=%fused_computation.14 | convolution fusion | flops 839024640 | bytes 8193536 | tf_op jit(solution)/shard_map/dot_general | solution.py:38
  80.5 17.1 %multiply_add_fusion = (f32[640,2560]{1,0:T(8,128)}, bf16[1,640,2560]{2,1,0:T(8,128)(2,1)}, bf16[1,640,2560]{2,1,0:T(8,128)(2,1)}, bf16[1,640,2560]{2,1,0:T(8,128)(2,1)}, bf16[1,640,2560]{2,1,0:T(8,128)(2,1)}) fusion(f32[640,2560]{1,0:T(8,128)} %fusion.4, f32[640,2560]{1,0:T(8,128)S(1)} %fusion.6, f32[640,2560]{1,0:T(8,128)} %fusion.8, ...), kind=kOutput, calls=%fused_computation.4 | convolution fusion | flops 857047040 | bytes 40961536 | tf_op jit(solution)/shard_map/dot_general | solution.py:38
  97.6 0.0 all-reduce.2.cloned.1.call-update
  97.6 2.8 %convolution_convert_fusion.2 = bf16[128,640]{1,0:T(8,128)(2,1)S(1)} fusion(bf16[128,2560]{1,0:T(8,128)(2,1)} %param.10, bf16[2560,640]{1,0:T(8,128)(2,1)} %param.12), kind=kOutput, calls=%fused_computation.22 | convolution fusion | flops 419512320 | bytes 4096000 | tf_op jit(solution)/shard_map/dot_general | solution.py:12
  100.5 17.4 %all_gather.6 = bf16[128,2560]{1,0:T(8,128)(2,1)} all-gather(bf16[128,640]{1,0:T(8,128)(2,1)S(1)} %convolution_convert_fusion.2), channel_id=1, replica_groups=mesh['dp'=8,'mp'=4] {'mp'}, dimensions={1}, use_global_device_ids=true | all-gather | bytes 819200 | tf_op jit(solution)/shard_map/all_gather | solution.py:23
  117.9 85.4 %all-reduce.2.cloned.1.call-done = f32[640,2560]{1,0:T(8,128)} async-done(((f32[640,2560]{1,0:T(8,128)}), f32[640,2560]{1,0:T(8,128)}) %all-reduce.2.cloned.1.call-update) | async-done | bytes 6553616 | tf_op jit(solution)/shard_map/psum | solution.py:46
  203.3 5.3 %multiply_reduce_fusion = f32[]{:T(128)} fusion(f32[640,2560]{1,0:T(8,128)} %all-reduce.2.cloned.1.call-done), kind=kLoop, calls=%fused_computation.6 | loop fusion | flops 3276799 | bytes 6553604 | tf_op jit(solution)/shard_map/reduce_sum | solution.py:47
  208.6 8.7 %pad_maximum_fusion = bf16[4,640,2560]{2,1,0:T(8,128)(2,1)} fusion(bf16[1,640,2560]{2,1,0:T(8,128)(2,1)} %get-tuple-element.9, bf16[1,640,2560]{2,1,0:T(8,128)(2,1)} %get-tuple-element.8, bf16[1,640,2560]{2,1,0:T(8,128)(2,1)S(1)} %copy-done.2, bf16[1,640,2560]{2,1,0:T(8,128)(2,1)S(1)} %copy-done.1), kind=kLoop, calls=%fused_computation | loop fusion | flops 19660800 | bytes 26214400 | tf_op jit(solution)/shard_map/stack | solution.py:43
  217.3 12.5 %psum.22 = f32[]{:T(128)} all-reduce(f32[]{:T(128)} %multiply_reduce_fusion), channel_id=1, replica_groups=mesh['dp'=8,'mp'=4] {'mp'}, use_global_device_ids=true, to_apply=%region_3.4 | all-reduce | flops 1 | bytes 8 | tf_op jit(solution)/shard_map/psum | solution.py:47
  230.5 6.7 %fusion.3 = bf16[640,2560,1]{1,0,2:T(8,128)(2,1)} fusion(f32[640,2560]{1,0:T(8,128)} %all-reduce.2.cloned.1.call-done, bf16[128,2560]{1,0:T(8,128)(2,1)} %all_gather.6, f32[]{:T(128)S(6)} %div.7, bf16[128,2560]{1,0:T(8,128)(2,1)} %param.11, bf16[2560,640]{1,0:T(8,128)(2,1)S(1)} %copy-done), kind=kOutput, calls=%fused_computation.7 | convolution fusion | flops 845496320 | bytes 14417924 | tf_op jit(solution)/shard_map/qti,qtj->qij/dot_general | solution.py:49
  237.1 23.7 %fusion.12 = f32[1,4]{1,0:T(1,128)S(1)} fusion(bf16[4,640,2560]{2,1,0:T(8,128)(2,1)} %pad_maximum_fusion, bf16[640,2560,1]{1,0,2:T(8,128)(2,1)} %fusion.3), kind=kOutput, calls=%fused_computation.24 | convolution fusion | flops 13107200 | bytes 16384016 | tf_op jit(solution)/shard_map/qik,sik->qs/dot_general | solution.py:53
  260.9 8.9 %psum.23 = f32[1,4]{1,0:T(1,128)} all-reduce(f32[1,4]{1,0:T(1,128)S(1)} %fusion.12), channel_id=1, replica_groups=mesh['dp'=8,'mp'=4] {'mp'}, use_global_device_ids=true, to_apply=%region_4.5 | all-reduce | flops 4 | bytes 32 | tf_op jit(solution)/shard_map/psum | solution.py:54
  (8 shorter events, 0.0 us)
Async XLA Ops:
  6.5 15.0 %copy-start = (bf16[2560,640]{1,0:T(8,128)(2,1)S(1)}, bf16[2560,640]{1,0:T(8,128)(2,1)}, u32[]{:S(2)}) copy-start(bf16[2560,640]{1,0:T(8,128)(2,1)} %param.13) | copy-start | bytes 9830404
  6.5 6.0 %copy-start.5 = (s32[4]{0:T(128)S(1)}, s32[4]{0:T(128)}, u32[]{:S(2)}) copy-start(s32[4]{0:T(128)} %param.9) | copy-start | bytes 52
  6.5 63.4 %all-gather.2.cloned.1.call-start = ((), (), s32[]{:S(2)}) async-start(), calls=%async_computation | async-start | bytes 3276800 | tf_op jit(solution)/shard_map/all_gather | solution.py:22
  12.5 190.8 %all-reduce.2.cloned.1.call-start = ((), (), s32[]{:S(2)}) async-start(), calls=%async_computation.1 | async-start | bytes 13107200 | tf_op jit(solution)/shard_map/psum | solution.py:46
  69.9 2.8 copy-start.3
  69.9 2.8 copy-start.4
  203.3 5.3 %copy-start.1 = (bf16[1,640,2560]{2,1,0:T(8,128)(2,1)S(1)}, bf16[1,640,2560]{2,1,0:T(8,128)(2,1)}, u32[]{:S(2)}) copy-start(bf16[1,640,2560]{2,1,0:T(8,128)(2,1)} %get-tuple-element.6) | copy-start | bytes 9830404
  203.3 5.3 %copy-start.2 = (bf16[1,640,2560]{2,1,0:T(8,128)(2,1)S(1)}, bf16[1,640,2560]{2,1,0:T(8,128)(2,1)}, u32[]{:S(2)}) copy-start(bf16[1,640,2560]{2,1,0:T(8,128)(2,1)} %get-tuple-element.7) | copy-start | bytes 9830404
Sparse Core Ops, SparseCore 0:
  12.6 57.2 all-gather.1
  97.8 105.4 all-reduce.1
where the time goes:
time: 277 us
  waiting for transfers between devices  129 us (47%)
  matrix products  71.8 us (26%)
  blocking collectives  38.7 us (14%)
  other arithmetic  19.2 us (7%)
  between operations  16.6 us (6%)
    psum x1, waiting for transfers between devices, shards(): curvature = lax.psum(curvature_local, 'dp') * inverse_count  85.4 us
    all_gather x1, waiting for transfers between devices, shards(): lax.all_gather(acts_block, 'mp', axis=1, tiled=True)  43.4 us
    dot_general x4, matrix products, shards(): lax.dot_general(grads_win, acts_win, (((0,), (0,)), ((), ())), preferred_...  27.7 us
    dot_general x1, matrix products, shards(): jnp.einsum('qik,sik->qs', precond, stored, preferred_element_type=jnp.flo...  23.7 us
    all_gather x1, blocking collectives, shards(): lax.all_gather(query_block, 'mp', axis=1, tiled=True)  17.4 us
    dot_general x3, matrix products, rotate(): jnp.dot(values, basis, preferred_element_type=jnp.float32)  13.7 us
    psum x1, blocking collectives, shards(): grand_total = lax.psum(jnp.sum(curvature), 'mp')  12.5 us
    psum x1, blocking collectives, shards(): return lax.psum(partial_value, 'mp')  8.86 us
  transfers between devices with their start and end apart: 2, of which 2 were waited for; matrix products, arithmetic and copies ran while one was open for 5% of the time, Pallas kernels for 0%

commit v1 on v0

--- a/solution.py
+++ b/solution.py
@@ -43,7 +43,7 @@
     stored = jnp.stack(stored_list)
     inverse_count = 1.0 / (slot_count * lax.axis_size("dp"))
     query_full = query_rot.reshape(QUERIES, QLEN, -1)
-    curvature = lax.psum(curvature_local, "dp") * inverse_count
+    curvature = jnp.sum(lax.all_gather(curvature_local, "dp"), axis=0) * inverse_count
     grand_total = lax.psum(jnp.sum(curvature), "mp")
     damping = damping_ratio * grand_total / (curvature.size * lax.axis_size("mp"))
     local_grad = jnp.einsum(

time: 277 us -> 434 us (1.57)
  waiting for transfers between devices: 129 us -> 263 us
  other arithmetic: 19.2 us -> 42.1 us
    all_gather x0 -> x1, waiting for transfers between devices: none -> 219 us  [shards(): lax.all_gather(curvature_local, 'dp')]
    psum x1 -> x0, waiting for transfers between devices: 85.4 us -> none  [shards(): curvature = lax.psum(curvature_local, 'dp') * inverse_count]
    reduce_sum x0 -> x1, other arithmetic: none -> 22.9 us  [shards(): jnp.sum(lax.all_gather(curvature_local, 'dp'), axis=0) * inverse_count]
  transfers between devices with their start and end apart: 2 -> 2, of which waited for: 2 -> 2; matrix products, arithmetic and copies ran while one was open for 5% -> 3% of each run, Pallas kernels for 0% -> 0%
where the time goes in v1:
time: 434 us
  waiting for transfers between devices  263 us (61%)
  matrix products  71.8 us (17%)
  other arithmetic  42.1 us (10%)
  blocking collectives  38.8 us (9%)
  between operations  16.6 us (4%)
    all_gather x1, waiting for transfers between devices, shards(): lax.all_gather(curvature_local, 'dp')  219 us
    all_gather x1, waiting for transfers between devices, shards(): lax.all_gather(acts_block, 'mp', axis=1, tiled=True)  43.4 us
    dot_general x4, matrix products, shards(): lax.dot_general(grads_win, acts_win, (((0,), (0,)), ((), ())), preferred_...  27.8 us
    dot_general x1, matrix products, shards(): jnp.einsum('qik,sik->qs', precond, stored, preferred_element_type=jnp.flo...  23.7 us
    reduce_sum x1, other arithmetic, shards(): jnp.sum(lax.all_gather(curvature_local, 'dp'), axis=0) * inverse_count  22.9 us
    all_gather x1, blocking collectives, shards(): lax.all_gather(query_block, 'mp', axis=1, tiled=True)  17.4 us
    dot_general x3, matrix products, rotate(): jnp.dot(values, basis, preferred_element_type=jnp.float32)  13.7 us
    psum x1, blocking collectives, shards(): grand_total = lax.psum(jnp.sum(curvature), 'mp')  12.5 us
  transfers between devices with their start and end apart: 2, of which 2 were waited for; matrix products, arithmetic and copies ran while one was open for 3% of the time, Pallas kernels for 0%

profile of v1, /device:TPU:0, one launch (start us, length us, event | category | flops | bytes accessed | tf_op | source)
XLA Modules:
  0.0 433.6 jit_solution(18284254138904770987)
XLA Ops:
  6.5 0.0 copy-start
  6.5 0.0 all-gather.4.cloned.1.call-start
  6.5 5.9 %convolution_convert_fusion = bf16[512,640]{1,0:T(8,128)(2,1)} fusion(bf16[512,2560]{1,0:T(8,128)(2,1)} %param.7, bf16[2560,640]{1,0:T(8,128)(2,1)} %param.12), kind=kOutput, calls=%fused_computation.12 | convolution fusion | flops 1678049280 | bytes 6553600 | tf_op jit(solution)/shard_map/dot_general | solution.py:12
  12.4 0.0 all-gather.4.cloned.1.call-update
  12.5 0.0 all-gather.6.cloned.1.call-start
  12.5 0.0 copy-done.5
  12.5 0.2 reduce-window.4
  12.7 0.6 fusion.42
  15.9 0.6 fusion.41
  16.5 1.2 compare_and_fusion
  17.7 1.3 compare_and_fusion.1
  19.0 1.3 compare_and_fusion.2
  20.2 1.3 compare_and_fusion.3
  21.5 0.0 copy-done
  21.5 5.0 %convolution_convert_fusion.1 = bf16[512,640]{1,0:T(8,128)(2,1)} fusion(bf16[512,2560]{1,0:T(8,128)(2,1)} %param.8, bf16[2560,640]{1,0:T(8,128)(2,1)S(1)} %copy-done), kind=kOutput, calls=%fused_computation.13 | convolution fusion | flops 1678049280 | bytes 6553600 | tf_op jit(solution)/shard_map/dot_general | solution.py:12
  26.5 43.4 %all-gather.4.cloned.1.call-done = bf16[512,2560]{1,0:T(8,128)(2,1)} async-done(((bf16[512,640]{1,0:T(8,128)(2,1)}), bf16[512,2560]{1,0:T(8,128)(2,1)}) %all-gather.4.cloned.1.call-update) | async-done | bytes 2621456 | tf_op jit(solution)/shard_map/all_gather | solution.py:22
  69.9 2.7 fusion.4
  72.7 0.0 copy-done.3
  72.7 3.9 fusion.6
  76.5 3.9 fusion.8
  80.4 17.3 %multiply_add_fusion = (f32[640,2560]{1,0:T(8,128)}, bf16[1,640,2560]{2,1,0:T(8,128)(2,1)}, bf16[1,640,2560]{2,1,0:T(8,128)(2,1)}, bf16[1,640,2560]{2,1,0:T(8,128)(2,1)}, bf16[1,640,2560]{2,1,0:T(8,128)(2,1)}) fusion(f32[640,2560]{1,0:T(8,128)S(1)} %fusion.4, f32[640,2560]{1,0:T(8,128)} %fusion.6, f32[640,2560]{1,0:T(8,128)} %fusion.8, ...), kind=kOutput, calls=%fused_computation.4 | convolution fusion | flops 857047040 | bytes 40961536 | tf_op jit(solution)/shard_map/dot_general | solution.py:38
  97.7 0.0 all-gather.6.cloned.1.call-update
  97.7 2.8 convolution_convert_fusion.2
  100.6 17.4 %all_gather.12 = bf16[128,2560]{1,0:T(8,128)(2,1)} all-gather(bf16[128,640]{1,0:T(8,128)(2,1)S(1)} %convolution_convert_fusion.2), channel_id=1, replica_groups=mesh['dp'=8,'mp'=4] {'mp'}, dimensions={1}, use_global_device_ids=true | all-gather | bytes 819200 | tf_op jit(solution)/shard_map/all_gather | solution.py:23
  118.0 219.5 %all-gather.6.cloned.1.call-done = f32[5120,2560]{1,0:T(8,128)} async-done(((f32[640,2560]{1,0:T(8,128)}), f32[5120,2560]{1,0:T(8,128)}) %all-gather.6.cloned.1.call-update) | async-done | bytes 52428816 | tf_op jit(solution)/shard_map/all_gather | solution.py:46
  337.4 22.9 %reduce_sum.18 = f32[640,2560]{1,0:T(8,128)} reduce(f32[8,640,2560]{2,1,0:T(8,128)} %bitcast.35, f32[]{:T(128)} %constant.6.clone.1), dimensions={0}, to_apply=%region_1.2 | reduce | flops 11468800 | bytes 58982404 | tf_op jit(solution)/shard_map/reduce_sum | solution.py:46
  360.4 5.3 %multiply_reduce_fusion = f32[]{:T(128)} fusion(f32[640,2560]{1,0:T(8,128)} %reduce_sum.18), kind=kLoop, calls=%fused_computation.6 | loop fusion | flops 3276799 | bytes 6553604 | tf_op jit(solution)/shard_map/reduce_sum | solution.py:47
  365.7 8.7 %pad_maximum_fusion = bf16[4,640,2560]{2,1,0:T(8,128)(2,1)} fusion(bf16[1,640,2560]{2,1,0:T(8,128)(2,1)} %get-tuple-element.9, bf16[1,640,2560]{2,1,0:T(8,128)(2,1)} %get-tuple-element.8, bf16[1,640,2560]{2,1,0:T(8,128)(2,1)S(1)} %copy-done.2, bf16[1,640,2560]{2,1,0:T(8,128)(2,1)S(1)} %copy-done.1), kind=kLoop, calls=%fused_computation | loop fusion | flops 19660800 | bytes 26214400 | tf_op jit(solution)/shard_map/stack | solution.py:43
  374.4 12.5 %psum.14 = f32[]{:T(128)} all-reduce(f32[]{:T(128)} %multiply_reduce_fusion), channel_id=1, replica_groups=mesh['dp'=8,'mp'=4] {'mp'}, use_global_device_ids=true, to_apply=%region_3.4 | all-reduce | flops 1 | bytes 8 | tf_op jit(solution)/shard_map/psum | solution.py:47
  387.5 6.6 %fusion.3 = bf16[640,2560,1]{1,0,2:T(8,128)(2,1)} fusion(f32[640,2560]{1,0:T(8,128)} %reduce_sum.18, bf16[128,2560]{1,0:T(8,128)(2,1)} %all_gather.12, f32[]{:T(128)S(6)} %div.7, bf16[128,2560]{1,0:T(8,128)(2,1)} %param.11, bf16[2560,640]{1,0:T(8,128)(2,1)S(1)} %copy-done), kind=kOutput, calls=%fused_computation.7 | convolution fusion | flops 845496320 | bytes 14417924 | tf_op jit(solution)/shard_map/qti,qtj->qij/dot_general | solution.py:49
  394.1 23.7 %fusion.12 = f32[1,4]{1,0:T(1,128)S(1)} fusion(bf16[4,640,2560]{2,1,0:T(8,128)(2,1)} %pad_maximum_fusion, bf16[640,2560,1]{1,0,2:T(8,128)(2,1)} %fusion.3), kind=kOutput, calls=%fused_computation.24 | convolution fusion | flops 13107200 | bytes 16384016 | tf_op jit(solution)/shard_map/qik,sik->qs/dot_general | solution.py:53
  417.9 8.9 %psum.15 = f32[1,4]{1,0:T(1,128)} all-reduce(f32[1,4]{1,0:T(1,128)S(1)} %fusion.12), channel_id=1, replica_groups=mesh['dp'=8,'mp'=4] {'mp'}, use_global_device_ids=true, to_apply=%region_4.5 | all-reduce | flops 4 | bytes 32 | tf_op jit(solution)/shard_map/psum | solution.py:54
  (9 shorter events, 0.0 us)
Async XLA Ops:
  6.5 15.0 %copy-start = (bf16[2560,640]{1,0:T(8,128)(2,1)S(1)}, bf16[2560,640]{1,0:T(8,128)(2,1)}, u32[]{:S(2)}) copy-start(bf16[2560,640]{1,0:T(8,128)(2,1)} %param.13) | copy-start | bytes 9830404
  6.5 6.0 %copy-start.5 = (s32[4]{0:T(128)S(1)}, s32[4]{0:T(128)}, u32[]{:S(2)}) copy-start(s32[4]{0:T(128)} %param.9) | copy-start | bytes 52
  6.5 63.4 %all-gather.4.cloned.1.call-start = ((), (), s32[]{:S(2)}) async-start(), calls=%async_computation | async-start | bytes 3276800 | tf_op jit(solution)/shard_map/all_gather | solution.py:22
  12.5 325.0 %all-gather.6.cloned.1.call-start = ((), (), s32[]{:S(2)}) async-start(), calls=%async_computation.1 | async-start | bytes 58982400 | tf_op jit(solution)/shard_map/all_gather | solution.py:46
  69.9 2.7 copy-start.3
  69.9 2.7 copy-start.4
  360.3 5.3 %copy-start.1 = (bf16[1,640,2560]{2,1,0:T(8,128)(2,1)S(1)}, bf16[1,640,2560]{2,1,0:T(8,128)(2,1)}, u32[]{:S(2)}) copy-start(bf16[1,640,2560]{2,1,0:T(8,128)(2,1)} %get-tuple-element.6) | copy-start | bytes 9830404
  360.4 5.3 %copy-start.2 = (bf16[1,640,2560]{2,1,0:T(8,128)(2,1)S(1)}, bf16[1,640,2560]{2,1,0:T(8,128)(2,1)}, u32[]{:S(2)}) copy-start(bf16[1,640,2560]{2,1,0:T(8,128)(2,1)} %get-tuple-element.7) | copy-start | bytes 9830404
Sparse Core Ops, SparseCore 0:
  12.6 57.2 all-gather.3
  97.9 239.5 all-gather.5
